TPU v7x, 256 devices: a whole 4x4x8 slice. The times are simulated.
256 devices in a mesh: group: 2 (over y_hi), dev: 128 (over y_lo, x, z, core).
Axes of the slice: x: 4, y: 4 (y_hi: 2, y_lo: 2; y = y_hi * 2 + y_lo), z: 8, core: 2. Of those that a mesh axis runs over, the one named last changes fastest.
Arguments:
- forces: float32 [3, 524288], P(None, ('group', 'dev')), may hold values from -4 to 4
- stencil_start: int32 [3, 524288], P(None, ('group', 'dev')), may hold values from 0 to 1023, as said below
- fraction: float32 [3, 524288], P(None, ('group', 'dev')), may hold values from 0 to 1
- tile_pairs: int32 [12288, 2], P(('group', 'dev')), may hold values from 0 to 15, as said below
- pair_count: int32 [256], P(('group', 'dev')), may hold values from 1 to 48, as said below
Outputs:
- velocity: float32 [3, 524288], P(None, ('group', 'dev'))
Inputs may be any that keep to these rules, and one draw needn't show every extreme that they name: `stencil_start`: along the first dimension, a point of block b = p // 2048 starts in planes b * 4 to (b + 1) * 4 - 1; along the others it lies in 0 to 127 and 0 to 127. `tile_pairs`: tile numbers are local to the device's block of 2048 points. `pair_count`: the live slots are the first ones of each device's list; some device has all 48 live.
All inputs are finite; a program needn't handle non-finite values.
Results may differ from a plain program's by a relative error of at most 0.0003.
Values sent between devices are 32-bit elements; how exact they have to be, the bound alone decides.
A program may use at most 64 MiB of HBM per device.

v0:
```python
import functools

import jax
import jax.numpy as jnp
import numpy as np
from jax import lax
from jax.experimental import pallas as pl
from jax.experimental.pallas import tpu as pltpu
from jax.sharding import PartitionSpec as P

NX = 1024
NY = 128
NZ = 128
MESH = pl.DeviceIdType.MESH
F32 = jnp.float32
BF16 = jnp.bfloat16
TWO_PI = 2.0 * np.pi
CHUNK = 256
VMEM = pltpu.VMEM
SLOTS = 48


def halves(table):
    table = np.asarray(table, np.float32)
    high = table.astype(BF16)
    low = (table - high.astype(np.float32)).astype(BF16)
    return jnp.asarray(high), jnp.asarray(low)


def make_tables():
    k = np.arange(64)[:, None]
    z = np.arange(128)[None, :]
    angle = TWO_PI * ((k * z) % 128) / 128
    forward_z = np.concatenate([np.cos(angle), -np.sin(angle)], 0)
    weight = np.where(k == 0, 1.0, 2.0) / float(NX * NY * NZ)
    back_z = np.concatenate([weight * np.cos(angle), -weight * np.sin(angle)], 0)
    n = np.arange(128)
    angle = TWO_PI * ((n[:, None] * n[None, :]) % 128) / 128
    table_y = np.concatenate([np.cos(angle), np.sin(angle)], 1)
    n = np.arange(256)
    angle = TWO_PI * ((n[:, None] * n[None, :]) % 256) / 256
    cosine, sine = np.cos(angle), np.sin(angle)
    forward_x = np.zeros((2, 256, 256, 2))
    forward_x[0, :, :, 0] = cosine
    forward_x[0, :, :, 1] = sine
    forward_x[1, :, :, 0] = -sine
    forward_x[1, :, :, 1] = cosine
    forward_x = forward_x.reshape(512, 512)
    mix = np.zeros((2, 4, 32, 2, 4, 32))
    for r in range(4):
        for x in range(4):
            factor = (-1j) ** (r * x)
            for lane in range(32):
                mix[0, x, lane, 0, r, lane] = round(factor.real)
                mix[0, x, lane, 1, r, lane] = round(factor.imag)
                mix[1, x, lane, 0, r, lane] = -round(factor.imag)
                mix[1, x, lane, 1, r, lane] = round(factor.real)
    mix = mix.reshape(256, 256)
    q = np.arange(256)[:, None]
    x = (np.arange(128) // 32)[None, :]
    angle = TWO_PI * ((q * x) % 1024) / 1024
    return dict(
        forward_z=halves(forward_z),
        back_z=halves(back_z),
        table_y=halves(table_y),
        forward_x=halves(forward_x),
        back_x=halves(forward_x.T),
        mix=jnp.asarray(mix.astype(BF16)),
        unmix=jnp.asarray(mix.T.astype(BF16)),
        turn=(jnp.asarray(np.cos(angle).astype(np.float32)), jnp.asarray(np.sin(angle).astype(np.float32))),
    )


def split(value):
    high = value.astype(BF16)
    low = (value - high.astype(F32)).astype(BF16)
    return high, low


def mm(a, b):
    return jnp.dot(a, b, preferred_element_type=F32)


def mm3(a, b):
    return mm(a[0], b[0]) + (mm(a[0], b[1]) + mm(a[1], b[0]))


def spline_weights(t):
    square = t * t
    cube = square * t
    rest = 1.0 - t
    return [
        rest * rest * rest / 6.0,
        (3.0 * cube - 6.0 * square + 4.0) / 6.0,
        (-3.0 * cube + 3.0 * square + 3.0 * t + 1.0) / 6.0,
        cube / 6.0,
    ]


def line_weights(start, weights, dim):
    rows = lax.broadcasted_iota(jnp.int32, (128, start.shape[1]), 0)
    at = (rows - start[dim : dim + 1]) & 127
    result = jnp.zeros(at.shape, F32)
    for j in range(4):
        result = jnp.where(at == j, weights[j][dim : dim + 1], result)
    return result


def plane_weights(start, weights, planes):
    offset = start[0:1] & 3
    result = []
    for plane in planes:
        total = jnp.zeros(offset.shape, F32)
        for j in range(4):
            total = jnp.where(offset + j == plane, weights[j][0:1], total)
        result.append(total)
    return result


def swap_blocks(a):
    lane = lax.broadcasted_iota(jnp.int32, a[0].shape, 1)
    wide = lane < 64
    narrow = (lane & 63) < 32
    b = [None] * 4
    for i in range(2):
        b[i] = jnp.where(wide, a[i], pltpu.roll(a[i + 2], 64, 1))
        b[i + 2] = jnp.where(wide, pltpu.roll(a[i], 64, 1), a[i + 2])
    o = [None] * 4
    for i in (0, 2):
        o[i] = jnp.where(narrow, b[i], pltpu.roll(b[i + 1], 32, 1))
        o[i + 1] = jnp.where(narrow, pltpu.roll(b[i], 96, 1), b[i + 1])
    return o


def spread_step(planes, stride, start_ref, fraction_ref, force_ref, table, acc, left_high, left_low):
    start = start_ref[...]
    weights = spline_weights(fraction_ref[...])
    force = force_ref[...]
    y = split(line_weights(start, weights, 1))
    right = jnp.concatenate(y, axis=0)
    z = mm3(table, split(line_weights(start, weights, 2)))
    along = plane_weights(start, weights, planes)
    count = len(planes)
    for c in range(3):
        for i in range(count):
            high, low = split(z * (force[c : c + 1] * along[i]))
            left_high[pl.ds((c * count + i) * 128, 128), :] = high
            left_low[pl.ds((c * count + i) * 128, 128), :] = low
    for c in range(3):
        rows = pl.ds(c * count * 128, count * 128)
        dims = (((1,), (1,)), ((), ()))
        acc[pl.ds(c * stride * 128, count * 128), :] += lax.dot_general(
            left_high[rows, :], right, dims, preferred_element_type=F32
        ) + lax.dot_general(left_low[rows, :], right, dims, preferred_element_type=F32)


def spread_own_kernel(start, fraction, force, fz_high, fz_low, out, acc, left_high, left_low):
    step = pl.program_id(0)

    @pl.when(step == 0)
    def _():
        acc[...] = jnp.zeros_like(acc)

    spread_step(range(4), 4, start, fraction, force, (fz_high[...], fz_low[...]), acc, left_high, left_low)

    @pl.when(step == pl.num_programs(0) - 1)
    def _():
        out[...] = acc[:, :128] + acc[:, 128:]


def spread_behind_kernel(
    start, fraction, force, fz_high, fz_low, own, ty_high, ty_low, out, acc, left_high, left_low
):
    step = pl.program_id(0)

    @pl.when(step == 0)
    def _():
        acc[:, :128] = own[...]
        acc[:, 128:] = jnp.zeros_like(own)

    spread_step(range(4, 7), 4, start, fraction, force, (fz_high[...], fz_low[...]), acc, left_high, left_low)

    @pl.when(step == pl.num_programs(0) - 1)
    def _():
        for c in range(3):
            parts = []
            for x in range(4):
                rows = pl.ds((c * 4 + x) * 128, 128)
                value = split(acc[rows, :128] + acc[rows, 128:])
                value = mm3(value, (ty_high[...], ty_low[...]))
                re, im = value[:64], value[64:]
                parts.append((re[:, :128] + im[:, 128:], im[:, :128] - re[:, 128:]))
            for part in range(2):
                blocks = swap_blocks([p[part] for p in parts])
                for q in range(4):
                    out[c, pl.ds(q * 128 + part, 64, stride=2), :] = blocks[q]


def point_spec():
    return pl.BlockSpec((3, CHUNK), lambda i: (0, i))


def whole(shape):
    return pl.BlockSpec(shape, lambda i: (0,) * len(shape))


def cost(flops):
    return pl.CostEstimate(flops=flops, bytes_accessed=4000000, transcendentals=0)


def spread_own(points, tables):
    steps = points[0].shape[1] // CHUNK
    return pl.pallas_call(
        spread_own_kernel,
        grid=(steps,),
        in_specs=[point_spec()] * 3 + [whole((128, 128))] * 2,
        out_specs=whole((1536, 128)),
        out_shape=jax.ShapeDtypeStruct((1536, 128), F32),
        scratch_shapes=[VMEM((1536, 256), F32), VMEM((1536, CHUNK), BF16), VMEM((1536, CHUNK), BF16)],
        cost_estimate=cost(4000000000),
        name="spread_own",
    )(*points, *tables["forward_z"])


def spread_behind(points, own, tables):
    steps = points[0].shape[1] // CHUNK
    return pl.pallas_call(
        spread_behind_kernel,
        grid=(steps,),
        in_specs=[point_spec()] * 3
        + [whole((128, 128))] * 2
        + [whole((1536, 128))]
        + [whole((128, 256))] * 2,
        out_specs=whole((3, 512, 128)),
        out_shape=jax.ShapeDtypeStruct((3, 512, 128), F32),
        scratch_shapes=[VMEM((1536, 256), F32), VMEM((1152, CHUNK), BF16), VMEM((1152, CHUNK), BF16)],
        cost_estimate=cost(4000000000),
        name="spread_behind",
    )(*points, *tables["forward_z"], own, *tables["table_y"])


def near_terms(tiles, terms):
    def slot(s, carry):
        row = tiles[s]
        col = tiles[SLOTS + s].T
        gap = []
        for d in range(3):
            whole_gap = row[d : d + 1] - col[:, d : d + 1]
            if d > 0:
                whole_gap = jnp.where(whole_gap > 64.0, whole_gap - 128.0, whole_gap)
                whole_gap = jnp.where(whole_gap < -64.0, whole_gap + 128.0, whole_gap)
            gap.append(whole_gap + (row[3 + d : 4 + d] - col[:, 3 + d : 4 + d]))
        distance = gap[0] * gap[0] + gap[1] * gap[1] + gap[2] * gap[2]
        inverse = lax.rsqrt(distance + 1.0)
        fall = 0.25 * jnp.exp(distance * (-1.0 / 16.0)) * (inverse * inverse * inverse)
        pulled = [col[:, 6 + c : 7 + c] for c in range(3)]
        along = (gap[0] * pulled[0] + gap[1] * pulled[1] + gap[2] * pulled[2]) * fall
        diagonal = (distance + 2.0) * fall
        for c in range(3):
            term = diagonal * pulled[c] + along * gap[c]
            terms[c, pl.ds(s, 1), :] = jnp.sum(term, axis=0, keepdims=True)
        return carry

    lax.fori_loop(0, SLOTS, slot, 0)


def exchange_kernel(
    send, fx_high, fx_low, bx_high, bx_low, mix, unmix, turn_cos, turn_sin, tiles,
    out, terms, mid_a, held, back, mid_b, modes, send_sem, recv_sem, local_sem,
):
    me = lax.axis_index("group") * 128 + lax.axis_index("dev")
    yx = me >> 4
    zc = me & 15

    def at(yx_, zc_):
        index = yx_ * 16 + zc_
        return (index >> 7, index & 127)

    barrier = pltpu.get_barrier_semaphore()
    for j in range(1, 16):
        pl.semaphore_signal(barrier, inc=1, device_id=at(yx, (zc + j) & 15), device_id_type=MESH)
        pl.semaphore_signal(barrier, inc=1, device_id=at((yx + j) & 15, zc), device_id_type=MESH)
    pl.semaphore_wait(barrier, 30)

    def phase(number, c, source, target, along_z):
        here = zc if along_z else yx
        pltpu.make_async_copy(source(here), target, local_sem.at[number, c]).start()
        for j in range(1, 16):
            there = (here + j) & 15
            pltpu.make_async_remote_copy(
                src_ref=source(there),
                dst_ref=target,
                send_sem=send_sem.at[number, c],
                recv_sem=recv_sem.at[number, c],
                device_id=at(yx, there) if along_z else at(there, zc),
                device_id_type=MESH,
            ).start()

    def finish(number, c, source, target, whole_source, whole_target):
        pltpu.make_async_copy(source, target, local_sem.at[number, c]).wait()
        everything = pltpu.make_async_remote_copy(
            src_ref=whole_source,
            dst_ref=whole_target,
            send_sem=send_sem.at[number, c],
            recv_sem=recv_sem.at[number, c],
            device_id=at(yx, zc),
            device_id_type=MESH,
        )
        everything.wait_recv()
        everything.wait_send()

    most = pl.ds(0, 15)
    for c in range(3):
        phase(0, c, lambda z, c=c: send.at[c, z], mid_a.at[c, zc], True)
    near_terms(tiles, terms)
    for c in range(3):
        finish(0, c, send.at[c, zc], mid_a.at[c, zc], send.at[c, most], mid_a.at[c, most])
        phase(1, c, lambda y, c=c: mid_a.at[c, :, y], held.at[c, yx], False)

    cos, sin = turn_cos[...], turn_sin[...]
    for c in range(3):
        finish(1, c, mid_a.at[c, :, yx], held.at[c, yx], held.at[c, most], held.at[c, most])
        value = split(held.reshape(3, 512, 128)[c])
        both = jnp.concatenate(value, axis=1)
        top = mm(fx_high[...], both)
        value = top[:, :128] + (top[:, 128:] + mm(fx_low[...], value[0]))
        re, im = value[:256], value[256:]
        turned = jnp.concatenate([re * cos + im * sin, im * cos - re * sin], axis=1)
        high, low = split(turned)
        modes[c] = mm(high, mix[...]) + mm(low, mix[...])

    column = zc * 16 + yx
    lane = lax.broadcasted_iota(jnp.int32, (256, 128), 1)
    row = lax.broadcasted_iota(jnp.int32, (256, 128), 0)
    index_x = row + 256 * (lane >> 5)
    index_y = (lane & 31) + 32 * (column >> 6)
    index_z = column & 63
    step_x = TWO_PI / NX
    step_y = TWO_PI / NY
    wave_x = jnp.where(index_x > 512, index_x - 1024, index_x).astype(F32) * step_x
    wave_y = jnp.where(index_y > 64, index_y - 128, index_y).astype(F32) * step_y
    wave_z = index_z.astype(F32) * step_y
    squared = wave_x * wave_x + wave_y * wave_y + wave_z * wave_z
    anchor = squared == 0.0
    drop = anchor | (index_x == 512) | (index_y == 64)
    inverse = jnp.where(drop, 0.0, 1.0 / jnp.where(anchor, 1.0, squared))
    waves = (wave_x, wave_y, wave_z)
    for part in range(2):
        lanes = slice(part * 128, part * 128 + 128)
        values = [modes[c, :, lanes] for c in range(3)]
        project = (wave_x * values[0] + wave_y * values[1] + wave_z * values[2]) * inverse
        for c in range(3):
            modes[c, :, lanes] = (values[c] - waves[c] * project) * inverse

    for c in range(3):
        high, low = split(modes[c])
        value = mm(high, unmix[...]) + mm(low, unmix[...])
        re, im = value[:, :128], value[:, 128:]
        value = split(jnp.concatenate([re * cos - im * sin, im * cos + re * sin], axis=0))
        both = jnp.concatenate(value, axis=1)
        top = mm(bx_high[...], both)
        back.reshape(3, 512, 128)[c] = top[:, :128] + (top[:, 128:] + mm(bx_low[...], value[0]))
        phase(2, c, lambda y, c=c: back.at[c, y], mid_b.at[c, yx], False)
    for c in range(3):
        finish(2, c, back.at[c, yx], mid_b.at[c, yx], back.at[c, most], mid_b.at[c, most])
        phase(3, c, lambda z, c=c: mid_b.at[c, :, z], out.at[c, zc], True)
    for c in range(3):
        finish(3, c, mid_b.at[c, :, zc], out.at[c, zc], out.at[c, most], out.at[c, most])


def exchange(send, tiles, tables):
    shape = (3, 16, 16, 2, 128)
    vmem = pl.BlockSpec(memory_space=pltpu.VMEM)
    return pl.pallas_call(
        exchange_kernel,
        in_specs=[vmem] * 10,
        out_specs=[vmem, vmem],
        out_shape=[jax.ShapeDtypeStruct(shape, F32), jax.ShapeDtypeStruct((3, SLOTS, 128), F32)],
        scratch_shapes=[VMEM(shape, F32)] * 4
        + [VMEM((3, 256, 256), F32)]
        + [pltpu.SemaphoreType.DMA((4, 3))] * 3,
        compiler_params=pltpu.CompilerParams(collective_id=0, has_side_effects=True),
        name="exchange",
    )(
        send.reshape(shape),
        *tables["forward_x"],
        *tables["back_x"],
        tables["mix"],
        tables["unmix"],
        *tables["turn"],
        tiles,
    )


def gather_step(planes, start_ref, fraction_ref, table, left, out):
    start = start_ref[...]
    weights = spline_weights(fraction_ref[...])
    y_high, y_low = split(line_weights(start, weights, 1))
    z = mm3(table, split(line_weights(start, weights, 2)))
    along = plane_weights(start, weights, planes)
    twice = jnp.concatenate([y_high, y_high], axis=0)
    for c in range(3):
        total = jnp.zeros_like(z)
        for i in range(len(planes)):
            rows = pl.ds((c * 4 + i) * 128, 128)
            both = left[rows, :]
            value = mm(both, twice) + mm(both[:, :128], y_low)
            total = total + value * along[i]
        out[c : c + 1, :] = jnp.sum(total * z, axis=0, keepdims=True)


def gather_behind_kernel(start, fraction, bz_high, bz_low, ty_high, ty_low, lines, out, left):
    @pl.when(pl.program_id(0) == 0)
    def _():
        for c in range(3):
            parts = []
            for part in range(2):
                parts.append(
                    swap_blocks([lines[c, pl.ds(q * 128 + part, 64, stride=2), :] for q in range(4)])
                )
            for x in range(4):
                value = split(jnp.concatenate([parts[0][x], parts[1][x]], axis=0))
                value = mm3(value, (ty_high[...], ty_low[...]))
                re, im = value[:64], value[64:]
                plane = jnp.concatenate([re[:, :128] - im[:, 128:], im[:, :128] + re[:, 128:]], axis=0)
                left[pl.ds((c * 4 + x) * 128, 128), :] = jnp.concatenate(split(plane), axis=1)

    gather_step(range(4, 7), start, fraction, (bz_high[...], bz_low[...]), left, out)


def gather_own_kernel(start, fraction, bz_high, bz_low, left, out):
    gather_step(range(4), start, fraction, (bz_high[...], bz_low[...]), left, out)


def gather_behind(points, lines, tables):
    count = points[0].shape[1]
    return pl.pallas_call(
        gather_behind_kernel,
        grid=(count // CHUNK,),
        in_specs=[point_spec()] * 2
        + [whole((128, 128))] * 2
        + [whole((128, 256))] * 2
        + [whole((3, 512, 128))],
        out_specs=[point_spec(), whole((1536, 256))],
        out_shape=[jax.ShapeDtypeStruct((3, count), F32), jax.ShapeDtypeStruct((1536, 256), BF16)],
        cost_estimate=cost(4000000000),
        name="gather_behind",
    )(*points[:2], *tables["back_z"], *tables["table_y"], lines)


def gather_own(points, left, tables):
    count = points[0].shape[1]
    return pl.pallas_call(
        gather_own_kernel,
        grid=(count // CHUNK,),
        in_specs=[point_spec()] * 2 + [whole((128, 128))] * 2 + [whole((1536, 256))],
        out_specs=point_spec(),
        out_shape=jax.ShapeDtypeStruct((3, count), F32),
        cost_estimate=cost(4000000000),
        name="gather_own",
    )(*points[:2], *tables["back_z"], left)


def from_behind(x, by):
    return lax.ppermute(x, ("group", "dev"), [(i, (i + by) % 256) for i in range(256)])


def per_device(tables, forces, stencil_start, fraction, tile_pairs, pair_count):
    count = forces.shape[1]
    tiles = count // 128
    own = (stencil_start, fraction, forces)
    start_float = stencil_start.astype(F32)
    packed = jnp.concatenate([start_float, fraction, forces], axis=0)
    behind = from_behind(packed, 1)
    behind = (behind[0:3].astype(jnp.int32), behind[3:6], behind[6:9])
    slab = spread_own(own, tables)
    send = spread_behind(behind, slab, tables)
    spots = jnp.arange(tiles, dtype=jnp.int32)[None, :]
    padded = jnp.concatenate([packed, jnp.zeros((7, count), F32)], axis=0)
    ends = (jnp.concatenate([tile_pairs[:, 0], tile_pairs[:, 1]])[:, None] == spots).astype(F32)
    picked = jnp.einsum(
        "st,ktp->skp", ends, padded.reshape(16, tiles, 128), precision=lax.Precision.HIGHEST
    )
    lines, terms = exchange(send, picked, tables)
    partial, left = gather_behind(behind, lines.reshape(3, 512, 128), tables)
    partial = from_behind(partial, -1)
    far = gather_own(own, left, tables)
    live = jnp.arange(SLOTS, dtype=jnp.int32) < pair_count[0]
    onehot = jnp.where(live[:, None], ends[:SLOTS], 0.0)
    near = jnp.einsum("st,csp->ctp", onehot, terms, precision=lax.Precision.HIGHEST)
    return far + near.reshape(3, count) + partial


def solution(mesh):
    tables = make_tables()
    in_specs = (
        P(None, ("group", "dev")),
        P(None, ("group", "dev")),
        P(None, ("group", "dev")),
        P(("group", "dev"), None),
        P(("group", "dev")),
    )
    return jax.shard_map(
        functools.partial(per_device, tables),
        mesh=mesh,
        in_specs=in_specs,
        out_specs=P(None, ("group", "dev")),
        check_vma=False,
    )
```

profile of v0, /device:TPU:1, one launch (start us, length us, event | category | flops | bytes accessed | tf_op | source)
XLA Modules:
  0.0 110.0 jit_solution(125182395690011163)
XLA Ops:
  0.0 0.0 copy-start
  0.0 0.0 copy-start.1
  0.0 0.8 convert_element_type.7
  0.8 0.0 copy-done
  0.8 0.0 copy-done.1
  0.8 0.0 copy-start.4
  0.8 3.1 %collective-permute-start = (f32[9,2048]{1,0:T(8,128)S(1)}, f32[9,2048]{1,0:T(8,128)S(1)}, u32[]{:S(2)}, u32[]{:S(2)}) collective-permute-start(f32[9,2048]{1,0:T(8,128)S(1)} %pad_maximum_fusion), channel_id=1, source_target_pairs={{0,1},{1,2},{2,3},{3,4},{4,5},{5,6},{6,7},{7,8},{8,9},{9,10},{10,1... | collective-permute-start | bytes 221192 | tf_op jit(solution)/shard_map/ppermute | solution.py:465
  3.9 0.0 copy-done.4
  4.0 0.1 pad.3.clone
  4.0 0.1 maximum_bitcast_fusion
  4.1 0.1 pad_add_fusion
  4.2 0.5 fusion.5
  4.7 1.3 %copy.20.tiles = f32[96,16,128]{2,1,0:T(8,128)} copy(f32[96,16,128]{2,0,1:T(8,128)S(1)} %fusion.5) | data formatting | bytes 1572864 | tf_op jit(solution)/shard_map/st,ktp->skp/dot_general | solution.py:481
  6.7 9.0 %spread_own.1.own = f32[1536,128]{1,0:T(8,128)} custom-call(s32[3,2048]{1,0:T(4,128)} %start.3, f32[3,2048]{1,0:T(4,128)} %fraction.3, f32[3,2048]{1,0:T(4,128)} %force.1, bf16[128,128]{1,0:T(8,128)(2,1)} %constant.14.clone.fz_high, bf16[128,128]{1,0:T(8,128)(2,1)} %constant.32.clone.fz_low), custom_call_target="tpu_custom_call" | custom-call | flops 4000000000 | bytes 4000000 | tf_op jit(solution)/shard_map/spread_own/pallas_call | solution.py:213
  15.7 0.0 collective-permute-done
  15.7 0.6 fusion.10
  16.3 9.4 %spread_behind.1 = f32[3,512,128]{2,1,0:T(8,128)} custom-call(s32[3,2048]{1,0:T(4,128)} %get-tuple-element.15.start, f32[3,2048]{1,0:T(4,128)} %get-tuple-element.14.fraction, f32[3,2048]{1,0:T(4,128)} %get-tuple-element.13.force, bf16[128,128]{1,0:T(8,128)(2,1)} %constant.14.clone.fz_high, bf16[128,128]{1,0:T(8,128)(2,1)} %constant.32.clone.fz_low, ...), custom_call_target="tpu_custom_call" | custom-call | flops 4000000000 | bytes 4000000 | tf_op jit(solution)/shard_map/spread_behind/pallas_call | solution.py:227
  25.8 66.8 %exchange.1 = (f32[3,16,16,2,128]{4,3,2,1,0:T(2,128)}, f32[3,48,128]{2,1,0:T(8,128)}) custom-call(f32[3,16,16,2,128]{4,3,2,1,0:T(2,128)} %bitcast.26, bf16[512,512]{1,0:T(8,128)(2,1)} %constant.35.clone.fx_high, bf16[512,512]{1,0:T(8,128)(2,1)} %constant.36.clone.fx_low, bf16[512,512]{1,0:T(8,128)(2,1)} %constant.37.clone.bx_high, ...), custom_call_target="tpu_custom_call" | custom-call | tf_op jit(solution)/shard_map/exchange/pallas_call | solution.py:374
  92.6 8.2 %gather_behind.1 = (f32[3,2048]{1,0:T(4,128)}, bf16[1536,256]{1,0:T(8,128)(2,1)}) custom-call(s32[3,2048]{1,0:T(4,128)} %get-tuple-element.15.start, f32[3,2048]{1,0:T(4,128)} %get-tuple-element.14.fraction, bf16[128,128]{1,0:T(8,128)(2,1)} %constant.43.clone.bz_high, bf16[128,128]{1,0:T(8,128)(2,1)} %constant.44.clone.bz_low, ...), custom_call_target="tpu_custom_call" | custom-call | flops 4000000000 | bytes 4000000 | tf_op jit(solution)/shard_map/gather_behind/pallas_call | solution.py:437
  100.8 0.0 collective-permute-start.1
  100.8 0.0 copy-start.2
  100.8 7.9 %gather_own.1 = f32[3,2048]{1,0:T(4,128)} custom-call(s32[3,2048]{1,0:T(4,128)} %start.3, f32[3,2048]{1,0:T(4,128)} %fraction.3, bf16[128,128]{1,0:T(8,128)(2,1)} %constant.43.clone.bz_high, bf16[128,128]{1,0:T(8,128)(2,1)} %constant.44.clone.bz_low, bf16[1536,256]{1,0:T(8,128)(2,1)} %get-tuple-element.10.left), custom_call_target="tpu_custom_call" | custom-call | flops 4000000000 | bytes 4000000 | tf_op jit(solution)/shard_map/gather_own/pallas_call | solution.py:453
  108.6 0.0 copy-done.2
  108.6 0.0 copy-start.3
  108.6 0.2 convolution_bitcast_fusion
  108.8 0.0 collective-permute-done.1
  108.8 0.6 copy-done.3
  109.4 0.6 fusion
  (6 shorter events, 0.1 us)
Async XLA Ops:
  0.0 0.8 copy-start
  0.0 0.8 copy-start.1
  0.8 3.2 %copy-start.4 = (s32[48,2]{0,1:T(2,128)S(1)}, s32[48,2]{0,1:T(2,128)}, u32[]{:S(2)}) copy-start(s32[48,2]{0,1:T(2,128)} %param.22) | copy-start | bytes 1156
  0.8 14.9 %collective-permute-start = (f32[9,2048]{1,0:T(8,128)S(1)}, f32[9,2048]{1,0:T(8,128)S(1)}, u32[]{:S(2)}, u32[]{:S(2)}) collective-permute-start(f32[9,2048]{1,0:T(8,128)S(1)} %pad_maximum_fusion), channel_id=1, source_target_pairs={{0,1},{1,2},{2,3},{3,4},{4,5},{5,6},{6,7},{7,8},{8,9},{9,10},{10,1... | collective-permute-start | bytes 221192 | tf_op jit(solution)/shard_map/ppermute | solution.py:465
  100.8 8.1 %collective-permute-start.1 = (f32[3,2048]{1,0:T(4,128)}, f32[3,2048]{1,0:T(4,128)S(1)}, u32[]{:S(2)}, u32[]{:S(2)}) collective-permute-start(f32[3,2048]{1,0:T(4,128)} %get-tuple-element.12), channel_id=1, source_target_pairs={{0,255},{1,0},{2,1},{3,2},{4,3},{5,4},{6,5},{7,6},{8,7},{9,8},{10,... | collective-permute-start | bytes 73736 | tf_op jit(solution)/shard_map/ppermute | solution.py:465
  100.8 7.9 %copy-start.2 = (f32[3,48,128]{2,1,0:T(8,128)S(1)}, f32[3,48,128]{2,1,0:T(8,128)}, u32[]{:S(2)}) copy-start(f32[3,48,128]{2,1,0:T(8,128)} %get-tuple-element.11) | copy-start | bytes 221188
  108.6 0.8 copy-start.3
where the time goes:
time: 111 us; the launch traced here: 110 us
  Pallas kernels  101 us (91%)
  starting transfers between devices  3.1 us (3%)
  other arithmetic  2.25 us (2%)
  local copies, waits for them, and re-layouts  2.03 us (2%)
    pallas_call x1, Pallas kernels, exchange(): pl.pallas_call(exchange_kernel, in_specs=[vmem] * 10, out_specs=[vmem, vm...  66.8 us
    pallas_call x1, Pallas kernels, spread_behind(): pl.pallas_call(spread_behind_kernel, grid=(steps,), in_specs=[point_spec(...  9.41 us
    pallas_call x1, Pallas kernels, spread_own(): pl.pallas_call(spread_own_kernel, grid=(steps,), in_specs=[point_spec()]...  8.96 us
    pallas_call x1, Pallas kernels, gather_behind(): pl.pallas_call(gather_behind_kernel, grid=(count // CHUNK,), in_specs=[po...  8.15 us
    pallas_call x1, Pallas kernels, gather_own(): pl.pallas_call(gather_own_kernel, grid=(count // CHUNK,), in_specs=[point...  7.86 us
    ppermute x2, starting transfers between devices, from_behind(): lax.ppermute(x, ('group', 'dev'), [(i, (i + by) % 256) for i in range(256)])  3.1 us
  transfers between devices with their start and end apart: 2, of which 0 were waited for; matrix products, arithmetic and copies ran while one was open for 2% of the time, Pallas kernels for 15%

commit v1 on v0

v1 whole, which is shorter than its diff:
```python
import functools

import jax
import jax.numpy as jnp
import numpy as np
from jax import lax
from jax.experimental import pallas as pl
from jax.experimental.pallas import tpu as pltpu
from jax.sharding import PartitionSpec as P

NX = 1024
NY = 128
NZ = 128
MESH = pl.DeviceIdType.MESH
F32 = jnp.float32
BF16 = jnp.bfloat16
TWO_PI = 2.0 * np.pi
CHUNK = 512
VMEM = pltpu.VMEM
SLOTS = 48


def halves(table):
    table = np.asarray(table, np.float32)
    high = table.astype(BF16)
    low = (table - high.astype(np.float32)).astype(BF16)
    return jnp.asarray(high), jnp.asarray(low)


def make_tables():
    k = np.arange(64)[:, None]
    z = np.arange(128)[None, :]
    angle = TWO_PI * ((k * z) % 128) / 128
    forward_z = np.concatenate([np.cos(angle), -np.sin(angle)], 0)
    weight = np.where(k == 0, 1.0, 2.0) / float(NX * NY * NZ)
    back_z = np.concatenate([weight * np.cos(angle), -weight * np.sin(angle)], 0)
    n = np.arange(128)
    angle = TWO_PI * ((n[:, None] * n[None, :]) % 128) / 128
    table_y = np.concatenate([np.cos(angle), np.sin(angle)], 1)
    n = np.arange(256)
    angle = TWO_PI * ((n[:, None] * n[None, :]) % 256) / 256
    cosine, sine = np.cos(angle), np.sin(angle)
    forward_x = np.zeros((2, 256, 256, 2))
    forward_x[0, :, :, 0] = cosine
    forward_x[0, :, :, 1] = sine
    forward_x[1, :, :, 0] = -sine
    forward_x[1, :, :, 1] = cosine
    forward_x = forward_x.reshape(512, 512)
    mix = np.zeros((2, 4, 32, 2, 4, 32))
    for r in range(4):
        for x in range(4):
            factor = (-1j) ** (r * x)
            for lane in range(32):
                mix[0, x, lane, 0, r, lane] = round(factor.real)
                mix[0, x, lane, 1, r, lane] = round(factor.imag)
                mix[1, x, lane, 0, r, lane] = -round(factor.imag)
                mix[1, x, lane, 1, r, lane] = round(factor.real)
    mix = mix.reshape(256, 256)
    q = np.arange(256)[:, None]
    x = (np.arange(128) // 32)[None, :]
    angle = TWO_PI * ((q * x) % 1024) / 1024
    return dict(
        forward_z=halves(forward_z),
        back_z=halves(back_z),
        table_y=halves(table_y),
        forward_x=halves(forward_x),
        back_x=halves(forward_x.T),
        mix=jnp.asarray(mix.astype(BF16)),
        unmix=jnp.asarray(mix.T.astype(BF16)),
        turn=(jnp.asarray(np.cos(angle).astype(np.float32)), jnp.asarray(np.sin(angle).astype(np.float32))),
    )


def split(value):
    high = value.astype(BF16)
    low = (value - high.astype(F32)).astype(BF16)
    return high, low


def mm(a, b):
    return jnp.dot(a, b, preferred_element_type=F32)


def mm3(a, b):
    return mm(a[0], b[0]) + (mm(a[0], b[1]) + mm(a[1], b[0]))


def spline_weights(t):
    square = t * t
    cube = square * t
    rest = 1.0 - t
    return [
        rest * rest * rest / 6.0,
        (3.0 * cube - 6.0 * square + 4.0) / 6.0,
        (-3.0 * cube + 3.0 * square + 3.0 * t + 1.0) / 6.0,
        cube / 6.0,
    ]


def line_weights(start, weights, dim):
    rows = lax.broadcasted_iota(jnp.int32, (128, start.shape[1]), 0)
    at = (rows - start[dim : dim + 1]) & 127
    result = jnp.zeros(at.shape, F32)
    for j in range(4):
        result = jnp.where(at == j, weights[j][dim : dim + 1], result)
    return result


def plane_weights(start, weights, planes):
    offset = start[0:1] & 3
    result = []
    for plane in planes:
        total = jnp.zeros(offset.shape, F32)
        for j in range(4):
            total = jnp.where(offset + j == plane, weights[j][0:1], total)
        result.append(total)
    return result


def swap_blocks(a):
    lane = lax.broadcasted_iota(jnp.int32, a[0].shape, 1)
    wide = lane < 64
    narrow = (lane & 63) < 32
    b = [None] * 4
    for i in range(2):
        b[i] = jnp.where(wide, a[i], pltpu.roll(a[i + 2], 64, 1))
        b[i + 2] = jnp.where(wide, pltpu.roll(a[i], 64, 1), a[i + 2])
    o = [None] * 4
    for i in (0, 2):
        o[i] = jnp.where(narrow, b[i], pltpu.roll(b[i + 1], 32, 1))
        o[i + 1] = jnp.where(narrow, pltpu.roll(b[i], 96, 1), b[i + 1])
    return o


def prepare(start_ref, fraction_ref, table, y_pair, z_modes, along, planes):
    def step(k, carry):
        cols = pl.ds(pl.multiple_of(k * 256, 256), 256)
        start = start_ref[:, cols]
        weights = spline_weights(fraction_ref[:, cols])
        y_high, y_low = split(line_weights(start, weights, 1))
        y_pair[:128, cols] = y_high
        y_pair[128:, cols] = y_low
        z_modes[:, cols] = mm3(table, split(line_weights(start, weights, 2)))
        for i, row in enumerate(plane_weights(start, weights, planes)):
            along[i : i + 1, cols] = row
        return carry

    lax.fori_loop(0, start_ref.shape[1] // 256, step, 0)


def back_modes(start_ref, fraction_ref, table, z_modes):
    def step(k, carry):
        cols = pl.ds(pl.multiple_of(k * 256, 256), 256)
        weights = spline_weights(fraction_ref[:, cols])
        z_modes[:, cols] = mm3(table, split(line_weights(start_ref[:, cols], weights, 2)))
        return carry

    lax.fori_loop(0, start_ref.shape[1] // 256, step, 0)


def spread(c, count, force_ref, y_pair, z_modes, along, acc):
    def step(k, carry):
        cols = pl.ds(pl.multiple_of(k * CHUNK, CHUNK), CHUNK)
        z = z_modes[:, cols]
        right = y_pair[:, cols]
        force = force_ref[c : c + 1, cols]
        pieces = [split(z * (force * along[i : i + 1, cols])) for i in range(count)]
        high = jnp.concatenate([p[0] for p in pieces], axis=0)
        low = jnp.concatenate([p[1] for p in pieces], axis=0)
        dims = (((1,), (1,)), ((), ()))
        acc[c, : count * 128, :] += lax.dot_general(
            high, right, dims, preferred_element_type=F32
        ) + lax.dot_general(low, right, dims, preferred_element_type=F32)
        return carry

    lax.fori_loop(0, force_ref.shape[1] // CHUNK, step, 0)


def gather(c, count, y_pair, z_modes, along, left, out):
    def step(k, carry):
        cols = pl.ds(pl.multiple_of(k * CHUNK, CHUNK), CHUNK)
        pair = y_pair[:, cols]
        twice = jnp.concatenate([pair[:128], pair[:128]], axis=0)
        both = left[c, : count * 128, :]
        value = mm(both, twice) + mm(both[:, :128], pair[128:])
        total = value[:128] * along[0:1, cols]
        for i in range(1, count):
            total = total + value[i * 128 : i * 128 + 128] * along[i : i + 1, cols]
        out[c : c + 1, cols] = jnp.sum(total * z_modes[:, cols], axis=0, keepdims=True)
        return carry

    lax.fori_loop(0, out.shape[1] // CHUNK, step, 0)


def lines_forward(acc, c, table, send):
    parts = []
    for x in range(4):
        rows = pl.ds(x * 128, 128)
        value = mm3(split(acc[c, rows, :128] + acc[c, rows, 128:]), table)
        re, im = value[:64], value[64:]
        parts.append((re[:, :128] + im[:, 128:], im[:, :128] - re[:, 128:]))
    for part in range(2):
        blocks = swap_blocks([p[part] for p in parts])
        for q in range(4):
            send[c, pl.ds(q * 128 + part, 64, stride=2), :] = blocks[q]


def lines_back(lines, c, table, left):
    parts = []
    for part in range(2):
        parts.append(swap_blocks([lines[c, pl.ds(q * 128 + part, 64, stride=2), :] for q in range(4)]))
    for x in range(4):
        value = mm3(split(jnp.concatenate([parts[0][x], parts[1][x]], axis=0)), table)
        re, im = value[:64], value[64:]
        plane = jnp.concatenate([re[:, :128] - im[:, 128:], im[:, :128] + re[:, 128:]], axis=0)
        left[c, pl.ds(x * 128, 128), :] = jnp.concatenate(split(plane), axis=1)


def pick_tiles(ends, start_ref, fraction_ref, force_ref, by_tile, tiles):
    count = start_ref.shape[1] // 128
    flat = by_tile.reshape(count * 16, 128)
    for t in range(count):
        cols = slice(t * 128, t * 128 + 128)
        by_tile[t, 0:3, :] = start_ref[:, cols].astype(F32)
        by_tile[t, 3:6, :] = fraction_ref[:, cols]
        by_tile[t, 6:9, :] = force_ref[:, cols]
    target = tiles.reshape(2 * SLOTS * 16, 128)
    for k in range(9):
        target[pl.ds(k, 2 * SLOTS, stride=16), :] = jnp.dot(
            ends[...],
            flat[pl.ds(k, count, stride=16), :],
            precision=lax.Precision.HIGHEST,
            preferred_element_type=F32,
        )


def near_sum(live, terms, near):
    for c in range(3):
        value = lax.dot_general(
            live[...],
            terms[c],
            (((0,), (0,)), ((), ())),
            precision=lax.Precision.HIGHEST,
            preferred_element_type=F32,
        )
        for t in range(value.shape[0]):
            near[c : c + 1, t * 128 : t * 128 + 128] = value[t : t + 1]


def near_terms(tiles, terms):
    def slot(s, carry):
        row = tiles[s]
        col = tiles[SLOTS + s].T
        gap = []
        for d in range(3):
            whole_gap = row[d : d + 1] - col[:, d : d + 1]
            if d > 0:
                whole_gap = jnp.where(whole_gap > 64.0, whole_gap - 128.0, whole_gap)
                whole_gap = jnp.where(whole_gap < -64.0, whole_gap + 128.0, whole_gap)
            gap.append(whole_gap + (row[3 + d : 4 + d] - col[:, 3 + d : 4 + d]))
        distance = gap[0] * gap[0] + gap[1] * gap[1] + gap[2] * gap[2]
        inverse = lax.rsqrt(distance + 1.0)
        fall = 0.25 * jnp.exp(distance * (-1.0 / 16.0)) * (inverse * inverse * inverse)
        pulled = [col[:, 6 + c : 7 + c] for c in range(3)]
        along = (gap[0] * pulled[0] + gap[1] * pulled[1] + gap[2] * pulled[2]) * fall
        diagonal = (distance + 2.0) * fall
        for c in range(3):
            term = diagonal * pulled[c] + along * gap[c]
            terms[c, pl.ds(s, 1), :] = jnp.sum(term, axis=0, keepdims=True)
        return carry

    lax.fori_loop(0, SLOTS, slot, 0)


def step_kernel(
    start, fraction, force, ends, live, fz_high, fz_low, bz_high, bz_low, ty_high, ty_low,
    fx_high_far, fx_low_far, bx_high_far, bx_low_far, mix_far, unmix_far, cos_far, sin_far,
    out,
    start_b, fraction_b, force_b, y_pair, z_modes, along, acc, left, by_tile, tiles, terms, near,
    fx_high, fx_low, bx_high, bx_low, mix, unmix, turn_cos, turn_sin,
    send, mid_a, held, back, mid_b, lines, modes, partial, partial_in,
    send_sem, recv_sem, local_sem, table_sem, point_send, point_recv, last_send, last_recv,
):
    me = lax.axis_index("group") * 128 + lax.axis_index("dev")
    yx = me >> 4
    zc = me & 15

    def at(yx_, zc_):
        index = yx_ * 16 + zc_
        return (index >> 7, index & 127)

    def near_by(by):
        index = (me + by) & 255
        return (index >> 7, index & 127)

    barrier = pltpu.get_barrier_semaphore()
    for by in (1, 255):
        pl.semaphore_signal(barrier, inc=1, device_id=near_by(by), device_id_type=MESH)
    for j in range(1, 16):
        pl.semaphore_signal(barrier, inc=1, device_id=at(yx, (zc + j) & 15), device_id_type=MESH)
        pl.semaphore_signal(barrier, inc=1, device_id=at((yx + j) & 15, zc), device_id_type=MESH)

    table_copies = [
        pltpu.make_async_copy(source, target, table_sem.at[i])
        for i, (source, target) in enumerate(
            [
                (fx_high_far, fx_high), (fx_low_far, fx_low), (bx_high_far, bx_high), (bx_low_far, bx_low),
                (mix_far, mix), (unmix_far, unmix), (cos_far, turn_cos), (sin_far, turn_sin),
            ]
        )
    ]
    for copy in table_copies:
        copy.start()

    shape = (3, 16, 16, 2, 128)
    send_blocks, back_blocks, lines_blocks = send.reshape(shape), back.reshape(shape), lines.reshape(shape)
    most = pl.ds(0, 15)

    def phase(number, c, source, target, along_z):
        here = zc if along_z else yx
        pltpu.make_async_copy(source(here), target, local_sem.at[number, c]).start()
        for j in range(1, 16):
            there = (here + j) & 15
            pltpu.make_async_remote_copy(
                src_ref=source(there),
                dst_ref=target,
                send_sem=send_sem.at[number, c],
                recv_sem=recv_sem.at[number, c],
                device_id=at(yx, there) if along_z else at(there, zc),
                device_id_type=MESH,
            ).start()

    def finish(number, c, source, target, whole_source, whole_target):
        pltpu.make_async_copy(source, target, local_sem.at[number, c]).wait()
        everything = pltpu.make_async_remote_copy(
            src_ref=whole_source,
            dst_ref=whole_target,
            send_sem=send_sem.at[number, c],
            recv_sem=recv_sem.at[number, c],
            device_id=near_by(1),
            device_id_type=MESH,
        )
        everything.wait_recv()
        everything.wait_send()

    table_z = (fz_high[...], fz_low[...])
    table_y = (ty_high[...], ty_low[...])
    y_own, z_own, a_own = y_pair.at[0], z_modes.at[0], along.at[0]
    y_behind, z_behind, a_behind = y_pair.at[1], z_modes.at[1], along.at[1]

    acc[...] = jnp.zeros_like(acc)
    prepare(start, fraction, table_z, y_own, z_own, a_own, range(4))
    spread(0, 4, force, y_own, z_own, a_own, acc)
    pl.semaphore_wait(barrier, 32)
    points = [
        pltpu.make_async_remote_copy(
            src_ref=source,
            dst_ref=target,
            send_sem=point_send.at[i],
            recv_sem=point_recv.at[i],
            device_id=near_by(1),
            device_id_type=MESH,
        )
        for i, (source, target) in enumerate([(start, start_b), (fraction, fraction_b), (force, force_b)])
    ]
    for copy in points:
        copy.start()
    spread(1, 4, force, y_own, z_own, a_own, acc)
    for copy in points:
        copy.wait()
    prepare(start_b, fraction_b, table_z, y_behind, z_behind, a_behind, range(4, 7))
    for c in range(3):
        if c == 2:
            spread(2, 4, force, y_own, z_own, a_own, acc)
        spread(c, 3, force_b, y_behind, z_behind, a_behind, acc)
        lines_forward(acc, c, table_y, send)
        phase(0, c, lambda z, c=c: send_blocks.at[c, z], mid_a.at[c, zc], True)

    def half_way(c):
        finish(0, c, send_blocks.at[c, zc], mid_a.at[c, zc], send_blocks.at[c, most], mid_a.at[c, most])
        phase(1, c, lambda y, c=c: mid_a.at[c, :, y], held.at[c, yx], False)

    def line_modes(c):
        finish(1, c, mid_a.at[c, :, yx], held.at[c, yx], held.at[c, most], held.at[c, most])
        value = split(held.reshape(3, 512, 128)[c])
        both = jnp.concatenate(value, axis=1)
        top = mm(fx_high[...], both)
        value = top[:, :128] + (top[:, 128:] + mm(fx_low[...], value[0]))
        re, im = value[:256], value[256:]
        cos, sin = turn_cos[...], turn_sin[...]
        turned = jnp.concatenate([re * cos + im * sin, im * cos - re * sin], axis=1)
        high, low = split(turned)
        modes[c] = mm(high, mix[...]) + mm(low, mix[...])

    half_way(0)
    pick_tiles(ends, start, fraction, force, by_tile, tiles)
    near_terms(tiles, terms)
    for copy in table_copies:
        copy.wait()
    half_way(1)
    line_modes(0)
    near_sum(live, terms, near)
    back_modes(start, fraction, (bz_high[...], bz_low[...]), z_own)
    back_modes(start_b, fraction_b, (bz_high[...], bz_low[...]), z_behind)
    half_way(2)
    line_modes(1)
    line_modes(2)

    column = zc * 16 + yx
    lane = lax.broadcasted_iota(jnp.int32, (256, 128), 1)
    row = lax.broadcasted_iota(jnp.int32, (256, 128), 0)
    index_x = row + 256 * (lane >> 5)
    index_y = (lane & 31) + 32 * (column >> 6)
    index_z = column & 63
    step_x = TWO_PI / NX
    step_y = TWO_PI / NY
    wave_x = jnp.where(index_x > 512, index_x - 1024, index_x).astype(F32) * step_x
    wave_y = jnp.where(index_y > 64, index_y - 128, index_y).astype(F32) * step_y
    wave_z = index_z.astype(F32) * step_y
    squared = wave_x * wave_x + wave_y * wave_y + wave_z * wave_z
    anchor = squared == 0.0
    drop = anchor | (index_x == 512) | (index_y == 64)
    inverse = jnp.where(drop, 0.0, 1.0 / jnp.where(anchor, 1.0, squared))
    waves = (wave_x, wave_y, wave_z)
    for part in range(2):
        lanes = slice(part * 128, part * 128 + 128)
        values = [modes[c, :, lanes] for c in range(3)]
        project = (wave_x * values[0] + wave_y * values[1] + wave_z * values[2]) * inverse
        for c in range(3):
            modes[c, :, lanes] = (values[c] - waves[c] * project) * inverse

    for c in range(3):
        high, low = split(modes[c])
        value = mm(high, unmix[...]) + mm(low, unmix[...])
        re, im = value[:, :128], value[:, 128:]
        cos, sin = turn_cos[...], turn_sin[...]
        value = split(jnp.concatenate([re * cos - im * sin, im * cos + re * sin], axis=0))
        both = jnp.concatenate(value, axis=1)
        top = mm(bx_high[...], both)
        back[c] = top[:, :128] + (top[:, 128:] + mm(bx_low[...], value[0]))
        phase(2, c, lambda y, c=c: back_blocks.at[c, y], mid_b.at[c, yx], False)
    for c in range(3):
        finish(2, c, back_blocks.at[c, yx], mid_b.at[c, yx], back_blocks.at[c, most], mid_b.at[c, most])
        phase(3, c, lambda z, c=c: mid_b.at[c, :, z], lines_blocks.at[c, zc], True)

    last = pltpu.make_async_remote_copy(
        src_ref=partial,
        dst_ref=partial_in,
        send_sem=last_send,
        recv_sem=last_recv,
        device_id=near_by(255),
        device_id_type=MESH,
    )
    for c in range(3):
        finish(3, c, mid_b.at[c, :, zc], lines_blocks.at[c, zc], lines_blocks.at[c, most], lines_blocks.at[c, most])
        lines_back(lines, c, table_y, left)
        gather(c, 3, y_behind, z_behind, a_behind, left, partial)
        if c == 2:
            last.start()
        gather(c, 4, y_own, z_own, a_own, left, out)
    last.wait()
    out[...] = out[...] + near[...] + partial_in[...]


def step(forces, stencil_start, fraction, ends, live, tables):
    count = forces.shape[1]
    vmem = pl.BlockSpec(memory_space=pltpu.VMEM)
    far = pl.BlockSpec(memory_space=pl.ANY)
    blocks = (3, 16, 16, 2, 128)
    x_tables = [*tables["forward_x"], *tables["back_x"], tables["mix"], tables["unmix"], *tables["turn"]]
    dma = pltpu.SemaphoreType.DMA
    return pl.pallas_call(
        step_kernel,
        in_specs=[vmem] * 11 + [far] * 8,
        out_specs=vmem,
        out_shape=jax.ShapeDtypeStruct((3, count), F32),
        scratch_shapes=[
            VMEM((3, count), jnp.int32),
            VMEM((3, count), F32),
            VMEM((3, count), F32),
            VMEM((2, 256, count), BF16),
            VMEM((2, 128, count), F32),
            VMEM((2, 8, count), F32),
            VMEM((3, 512, 256), F32),
            VMEM((3, 512, 256), BF16),
            VMEM((count // 128, 16, 128), F32),
            VMEM((2 * SLOTS, 16, 128), F32),
            VMEM((3, SLOTS, 128), F32),
            VMEM((3, count), F32),
        ]
        + [VMEM(t.shape, t.dtype) for t in x_tables]
        + [
            VMEM((3, 512, 128), F32),
            VMEM(blocks, F32),
            VMEM(blocks, F32),
            VMEM((3, 512, 128), F32),
            VMEM(blocks, F32),
            VMEM((3, 512, 128), F32),
            VMEM((3, 256, 256), F32),
            VMEM((3, count), F32),
            VMEM((3, count), F32),
            dma((4, 3)),
            dma((4, 3)),
            dma((4, 3)),
            dma((8,)),
            dma((3,)),
            dma((3,)),
            dma,
            dma,
        ],
        compiler_params=pltpu.CompilerParams(collective_id=0, has_side_effects=True),
        name="step",
    )(
        stencil_start,
        fraction,
        forces,
        ends,
        live,
        *tables["forward_z"],
        *tables["back_z"],
        *tables["table_y"],
        *x_tables,
    )


def per_device(tables, forces, stencil_start, fraction, tile_pairs, pair_count):
    spots = jnp.arange(forces.shape[1] // 128, dtype=jnp.int32)[None, :]
    ends = (jnp.concatenate([tile_pairs[:, 0], tile_pairs[:, 1]])[:, None] == spots).astype(F32)
    used = jnp.arange(SLOTS, dtype=jnp.int32) < pair_count[0]
    live = jnp.where(used[:, None], ends[:SLOTS], 0.0)
    return step(forces, stencil_start, fraction, ends, live, tables)


def solution(mesh):
    tables = make_tables()
    in_specs = (
        P(None, ("group", "dev")),
        P(None, ("group", "dev")),
        P(None, ("group", "dev")),
        P(("group", "dev"), None),
        P(("group", "dev")),
    )
    return jax.shard_map(
        functools.partial(per_device, tables),
        mesh=mesh,
        in_specs=in_specs,
        out_specs=P(None, ("group", "dev")),
        check_vma=False,
    )
```

time: 111 us -> 98 us (0.88)
  Pallas kernels: 101 us -> 94.2 us
  starting transfers between devices: 3.1 us -> 0 us
  other arithmetic: 2.25 us -> 0.85 us
    pallas_call x5 -> x1, Pallas kernels: 101 us -> 94.2 us  [step(): pl.pallas_call(step_kernel, in_specs=[vmem] * 11 + [far] * 8, out_specs=v...]
    ppermute x2 -> x0, starting transfers between devices: 3.1 us -> none  [from_behind(): lax.ppermute(x, ('group', 'dev'), [(i, (i + by) % 256) for i in range(256)])]
    unnamed x11 -> x5, local copies, waits for them, and re-layouts: 0.62 us -> 2.04 us
    dot_general x1 -> x0, local copies, waits for them, and re-layouts: 1.34 us -> none  [per_device(): jnp.einsum('st,ktp->skp', ends, padded.reshape(16, tiles, 128), precision...]
  transfers between devices with their start and end apart: 2 -> 0, of which waited for: 0 -> 0; matrix products, arithmetic and copies ran while one was open for 2% -> 0% of each run, Pallas kernels for 15% -> 0%
where the time goes in v1:
time: 98 us; the launch traced here: 97.8 us
  Pallas kernels  94.2 us (96%)
  local copies, waits for them, and re-layouts  2.05 us (2%)
    pallas_call x1, Pallas kernels, step(): pl.pallas_call(step_kernel, in_specs=[vmem] * 11 + [far] * 8, out_specs=v...  94.2 us
    unnamed x5, local copies, waits for them, and re-layouts  2.04 us

profile of v1, /device:TPU:1, one launch (start us, length us, event | category | flops | bytes accessed | tf_op | source)
XLA Modules:
  0.0 97.8 jit_solution(879642206957765085)
XLA Ops:
  0.7 0.0 copy-start.1
  0.7 0.7 copy-done.1
  1.3 0.1 pad_add_fusion
  1.4 0.1 fusion.ends
  1.5 0.0 copy-start
  1.5 0.7 slice_select_fusion.live
  2.2 0.0 copy-done
  2.2 94.2 %step.1 = f32[3,2048]{1,0:T(4,128)} custom-call(s32[3,2048]{1,0:T(4,128)} %start.1, f32[3,2048]{1,0:T(4,128)} %fraction.1, f32[3,2048]{1,0:T(4,128)} %force.1, f32[96,16]{1,0:T(8,128)} %copy-done, f32[48,16]{1,0:T(8,128)} %slice_select_fusion.live, bf16[128,128]{1,0:T(8,128)(2,1)} %constant.30.clone.fz_high, bf16[128,128]{1,0:T(8,128)(2,1)} %constant.31.clone.fz_low, ...), custom_call_target="tpu_custom_call" | custom-call | tf_op jit(solution)/shard_map/step/pallas_call | solution.py:472
  96.4 1.4 %copy.22 = f32[3,2048]{1,0:T(4,128)} copy(f32[3,2048]{1,0:T(4,128)} %step.1) | data formatting | bytes 49152
  (2 shorter events, 0.0 us)
Async XLA Ops:
  0.7 0.7 copy-start.1
  1.5 0.7 copy-start

commit v2 on v1

--- a/solution.py
+++ b/solution.py
@@ -18,6 +18,7 @@
 CHUNK = 512
 VMEM = pltpu.VMEM
 SLOTS = 48
+LOG2_E = 1.4426950408889634
 
 
 def halves(table):
@@ -64,7 +65,6 @@
         back_z=halves(back_z),
         table_y=halves(table_y),
         forward_x=halves(forward_x),
-        back_x=halves(forward_x.T),
         mix=jnp.asarray(mix.astype(BF16)),
         unmix=jnp.asarray(mix.T.astype(BF16)),
         turn=(jnp.asarray(np.cos(angle).astype(np.float32)), jnp.asarray(np.sin(angle).astype(np.float32))),
@@ -145,7 +145,7 @@
             along[i : i + 1, cols] = row
         return carry
 
-    lax.fori_loop(0, start_ref.shape[1] // 256, step, 0)
+    lax.fori_loop(0, start_ref.shape[1] // 256, step, 0, unroll=2)
 
 
 def back_modes(start_ref, fraction_ref, table, z_modes):
@@ -155,7 +155,7 @@
         z_modes[:, cols] = mm3(table, split(line_weights(start_ref[:, cols], weights, 2)))
         return carry
 
-    lax.fori_loop(0, start_ref.shape[1] // 256, step, 0)
+    lax.fori_loop(0, start_ref.shape[1] // 256, step, 0, unroll=2)
 
 
 def spread(c, count, force_ref, y_pair, z_modes, along, acc):
@@ -226,28 +226,23 @@
         by_tile[t, 6:9, :] = force_ref[:, cols]
     target = tiles.reshape(2 * SLOTS * 16, 128)
     for k in range(9):
-        target[pl.ds(k, 2 * SLOTS, stride=16), :] = jnp.dot(
-            ends[...],
+        target[pl.ds(k, 2 * SLOTS, stride=16), :] = lax.dot_general(
+            ends,
             flat[pl.ds(k, count, stride=16), :],
-            precision=lax.Precision.HIGHEST,
-            preferred_element_type=F32,
-        )
-
-
-def near_sum(live, terms, near):
-    for c in range(3):
-        value = lax.dot_general(
-            live[...],
-            terms[c],
             (((0,), (0,)), ((), ())),
             precision=lax.Precision.HIGHEST,
             preferred_element_type=F32,
         )
+
+
+def near_sum(live, terms, near):
+    for c in range(3):
+        value = jnp.dot(live, terms[c], precision=lax.Precision.HIGHEST, preferred_element_type=F32)
         for t in range(value.shape[0]):
             near[c : c + 1, t * 128 : t * 128 + 128] = value[t : t + 1]
 
 
-def near_terms(tiles, terms):
+def near_terms(tiles, terms, first, last):
     def slot(s, carry):
         row = tiles[s]
         col = tiles[SLOTS + s].T
@@ -260,7 +255,7 @@
             gap.append(whole_gap + (row[3 + d : 4 + d] - col[:, 3 + d : 4 + d]))
         distance = gap[0] * gap[0] + gap[1] * gap[1] + gap[2] * gap[2]
         inverse = lax.rsqrt(distance + 1.0)
-        fall = 0.25 * jnp.exp(distance * (-1.0 / 16.0)) * (inverse * inverse * inverse)
+        fall = jnp.exp2(distance * (-0.0625 * LOG2_E)) * (0.25 * inverse * inverse * inverse)
         pulled = [col[:, 6 + c : 7 + c] for c in range(3)]
         along = (gap[0] * pulled[0] + gap[1] * pulled[1] + gap[2] * pulled[2]) * fall
         diagonal = (distance + 2.0) * fall
@@ -269,16 +264,16 @@
             terms[c, pl.ds(s, 1), :] = jnp.sum(term, axis=0, keepdims=True)
         return carry
 
-    lax.fori_loop(0, SLOTS, slot, 0)
+    lax.fori_loop(first, last, slot, 0, unroll=2)
 
 
 def step_kernel(
-    start, fraction, force, ends, live, fz_high, fz_low, bz_high, bz_low, ty_high, ty_low,
-    fx_high_far, fx_low_far, bx_high_far, bx_low_far, mix_far, unmix_far, cos_far, sin_far,
-    out,
+    start, fraction, force, pairs, used, fz_high, fz_low, bz_high, bz_low, ty_high, ty_low,
+    fx_high_far, fx_low_far, mix_far, unmix_far, cos_far, sin_far,
+    out, partial_in,
     start_b, fraction_b, force_b, y_pair, z_modes, along, acc, left, by_tile, tiles, terms, near,
-    fx_high, fx_low, bx_high, bx_low, mix, unmix, turn_cos, turn_sin,
-    send, mid_a, held, back, mid_b, lines, modes, partial, partial_in,
+    fx_high, fx_low, mix, unmix, turn_cos, turn_sin, bx_high, bx_low,
+    send, mid_a, held, back, mid_b, lines, modes, partial,
     send_sem, recv_sem, local_sem, table_sem, point_send, point_recv, last_send, last_recv,
 ):
     me = lax.axis_index("group") * 128 + lax.axis_index("dev")
@@ -304,7 +299,7 @@
         pltpu.make_async_copy(source, target, table_sem.at[i])
         for i, (source, target) in enumerate(
             [
-                (fx_high_far, fx_high), (fx_low_far, fx_low), (bx_high_far, bx_high), (bx_low_far, bx_low),
+                (fx_high_far, fx_high), (fx_low_far, fx_low),
                 (mix_far, mix), (unmix_far, unmix), (cos_far, turn_cos), (sin_far, turn_sin),
             ]
         )
@@ -348,9 +343,6 @@
     y_own, z_own, a_own = y_pair.at[0], z_modes.at[0], along.at[0]
     y_behind, z_behind, a_behind = y_pair.at[1], z_modes.at[1], along.at[1]
 
-    acc[...] = jnp.zeros_like(acc)
-    prepare(start, fraction, table_z, y_own, z_own, a_own, range(4))
-    spread(0, 4, force, y_own, z_own, a_own, acc)
     pl.semaphore_wait(barrier, 32)
     points = [
         pltpu.make_async_remote_copy(
@@ -365,13 +357,15 @@
     ]
     for copy in points:
         copy.start()
-    spread(1, 4, force, y_own, z_own, a_own, acc)
+    acc[...] = jnp.zeros_like(acc)
+    prepare(start, fraction, table_z, y_own, z_own, a_own, range(4))
+    spread(0, 4, force, y_own, z_own, a_own, acc)
     for copy in points:
         copy.wait()
     prepare(start_b, fraction_b, table_z, y_behind, z_behind, a_behind, range(4, 7))
     for c in range(3):
-        if c == 2:
-            spread(2, 4, force, y_own, z_own, a_own, acc)
+        if c > 0:
+            spread(c, 4, force, y_own, z_own, a_own, acc)
         spread(c, 3, force_b, y_behind, z_behind, a_behind, acc)
         lines_forward(acc, c, table_y, send)
         phase(0, c, lambda z, c=c: send_blocks.at[c, z], mid_a.at[c, zc], True)
@@ -393,15 +387,19 @@
         modes[c] = mm(high, mix[...]) + mm(low, mix[...])
 
     half_way(0)
+    slot_tile = lax.broadcasted_iota(jnp.int32, (start.shape[1] // 128, SLOTS), 0)
+    ends = jnp.concatenate([jnp.where(slot_tile == pairs[e : e + 1, :], 1.0, 0.0) for e in range(2)], axis=1)
     pick_tiles(ends, start, fraction, force, by_tile, tiles)
-    near_terms(tiles, terms)
     for copy in table_copies:
         copy.wait()
+    bx_high[...] = fx_high[...].T
+    bx_low[...] = fx_low[...].T
+    near_terms(tiles, terms, 0, 12)
     half_way(1)
     line_modes(0)
-    near_sum(live, terms, near)
     back_modes(start, fraction, (bz_high[...], bz_low[...]), z_own)
     back_modes(start_b, fraction_b, (bz_high[...], bz_low[...]), z_behind)
+    near_terms(tiles, terms, 12, 16)
     half_way(2)
     line_modes(1)
     line_modes(2)
@@ -429,7 +427,7 @@
         for c in range(3):
             modes[c, :, lanes] = (values[c] - waves[c] * project) * inverse
 
-    for c in range(3):
+    def way_back(c):
         high, low = split(modes[c])
         value = mm(high, unmix[...]) + mm(low, unmix[...])
         re, im = value[:, :128], value[:, 128:]
@@ -438,10 +436,24 @@
         both = jnp.concatenate(value, axis=1)
         top = mm(bx_high[...], both)
         back[c] = top[:, :128] + (top[:, 128:] + mm(bx_low[...], value[0]))
-        phase(2, c, lambda y, c=c: back_blocks.at[c, y], mid_b.at[c, yx], False)
-    for c in range(3):
+        phase(2, c, lambda y: back_blocks.at[c, y], mid_b.at[c, yx], False)
+
+    def last_way(c):
         finish(2, c, back_blocks.at[c, yx], mid_b.at[c, yx], back_blocks.at[c, most], mid_b.at[c, most])
-        phase(3, c, lambda z, c=c: mid_b.at[c, :, z], lines_blocks.at[c, zc], True)
+        phase(3, c, lambda z: mid_b.at[c, :, z], lines_blocks.at[c, zc], True)
+
+    way_back(0)
+    way_back(1)
+    last_way(0)
+    way_back(2)
+    near_terms(tiles, terms, 16, 26)
+    last_way(1)
+    near_terms(tiles, terms, 26, 36)
+    last_way(2)
+    near_terms(tiles, terms, 36, SLOTS)
+    slot = lax.broadcasted_iota(jnp.int32, slot_tile.shape, 1)
+    live = jnp.where((slot_tile == pairs[0:1, :]) & (slot < used[0]), 1.0, 0.0)
+    near_sum(live, terms, near)
 
     last = pltpu.make_async_remote_copy(
         src_ref=partial,
@@ -459,21 +471,21 @@
             last.start()
         gather(c, 4, y_own, z_own, a_own, left, out)
     last.wait()
-    out[...] = out[...] + near[...] + partial_in[...]
-
-
-def step(forces, stencil_start, fraction, ends, live, tables):
+    out[...] = out[...] + near[...]
+
+
+def step(forces, stencil_start, fraction, tile_pairs, pair_count, tables):
     count = forces.shape[1]
     vmem = pl.BlockSpec(memory_space=pltpu.VMEM)
     far = pl.BlockSpec(memory_space=pl.ANY)
     blocks = (3, 16, 16, 2, 128)
-    x_tables = [*tables["forward_x"], *tables["back_x"], tables["mix"], tables["unmix"], *tables["turn"]]
+    x_tables = [*tables["forward_x"], tables["mix"], tables["unmix"], *tables["turn"]]
     dma = pltpu.SemaphoreType.DMA
     return pl.pallas_call(
         step_kernel,
-        in_specs=[vmem] * 11 + [far] * 8,
-        out_specs=vmem,
-        out_shape=jax.ShapeDtypeStruct((3, count), F32),
+        in_specs=[vmem] * 4 + [pl.BlockSpec(memory_space=pltpu.SMEM)] + [vmem] * 6 + [far] * 6,
+        out_specs=[vmem, vmem],
+        out_shape=[jax.ShapeDtypeStruct((3, count), F32)] * 2,
         scratch_shapes=[
             VMEM((3, count), jnp.int32),
             VMEM((3, count), F32),
@@ -489,6 +501,7 @@
             VMEM((3, count), F32),
         ]
         + [VMEM(t.shape, t.dtype) for t in x_tables]
+        + [VMEM((512, 512), BF16)] * 2
         + [
             VMEM((3, 512, 128), F32),
             VMEM(blocks, F32),
@@ -498,11 +511,10 @@
             VMEM((3, 512, 128), F32),
             VMEM((3, 256, 256), F32),
             VMEM((3, count), F32),
-            VMEM((3, count), F32),
             dma((4, 3)),
             dma((4, 3)),
             dma((4, 3)),
-            dma((8,)),
+            dma((6,)),
             dma((3,)),
             dma((3,)),
             dma,
@@ -514,8 +526,8 @@
         stencil_start,
         fraction,
         forces,
-        ends,
-        live,
+        tile_pairs.T,
+        pair_count,
         *tables["forward_z"],
         *tables["back_z"],
         *tables["table_y"],
@@ -524,11 +536,8 @@
 
 
 def per_device(tables, forces, stencil_start, fraction, tile_pairs, pair_count):
-    spots = jnp.arange(forces.shape[1] // 128, dtype=jnp.int32)[None, :]
-    ends = (jnp.concatenate([tile_pairs[:, 0], tile_pairs[:, 1]])[:, None] == spots).astype(F32)
-    used = jnp.arange(SLOTS, dtype=jnp.int32) < pair_count[0]
-    live = jnp.where(used[:, None], ends[:SLOTS], 0.0)
-    return step(forces, stencil_start, fraction, ends, live, tables)
+    far, behind = step(forces, stencil_start, fraction, tile_pairs, pair_count, tables)
+    return far + behind
 
 
 def solution(mesh):

time: 98 us -> 81 us (0.83)
  Pallas kernels: 94.2 us -> 78.8 us
  local copies, waits for them, and re-layouts: 2.05 us -> 0 us
    pallas_call x1, Pallas kernels: 94.2 us -> 78.8 us  [step(): pl.pallas_call(step_kernel, in_specs=[vmem] * 4 + [pl.BlockSpec(memory_sp...]
    unnamed x5 -> x0, local copies, waits for them, and re-layouts: 2.04 us -> none
    add x0 -> x1, other arithmetic: none -> 1.4 us  [per_device(): return far + behind]
where the time goes in v2:
time: 81 us; the launch traced here: 80.8 us
  Pallas kernels  78.8 us (97%)
  other arithmetic  1.4 us (2%)
    pallas_call x1, Pallas kernels, step(): pl.pallas_call(step_kernel, in_specs=[vmem] * 4 + [pl.BlockSpec(memory_sp...  78.8 us

profile of v2, /device:TPU:1, one launch (start us, length us, event | category | flops | bytes accessed | tf_op | source)
XLA Modules:
  0.0 80.8 jit_solution(8668302217342884028)
XLA Ops:
  0.7 78.8 %step.1 = (f32[3,2048]{1,0:T(4,128)}, f32[3,2048]{1,0:T(4,128)}) custom-call(s32[3,2048]{1,0:T(4,128)} %start.1, f32[3,2048]{1,0:T(4,128)} %fraction.1, f32[3,2048]{1,0:T(4,128)} %force.1, s32[2,48]{1,0:T(2,128)} %bitcast.1, s32[1]{0:T(128)S(6)} %copy.18.used, bf16[128,128]{1,0:T(8,128)(2,1)} %constant.24.clone.fz_high, ...), custom_call_target="tpu_custom_call" | custom-call | tf_op jit(solution)/shard_map/step/pallas_call | solution.py:484
  79.4 1.4 %add.3 = f32[3,2048]{1,0:T(4,128)} add(f32[3,2048]{1,0:T(4,128)} %get-tuple-element.7, f32[3,2048]{1,0:T(4,128)} %get-tuple-element.8) | non-fusion elementwise | flops 6144 | bytes 73728 | tf_op jit(solution)/shard_map/add | solution.py:540

commit v3 on v2

--- a/solution.py
+++ b/solution.py
@@ -173,7 +173,7 @@
         ) + lax.dot_general(low, right, dims, preferred_element_type=F32)
         return carry
 
-    lax.fori_loop(0, force_ref.shape[1] // CHUNK, step, 0)
+    lax.fori_loop(0, force_ref.shape[1] // CHUNK, step, 0, unroll=2)
 
 
 def gather(c, count, y_pair, z_modes, along, left, out):
@@ -189,7 +189,7 @@
         out[c : c + 1, cols] = jnp.sum(total * z_modes[:, cols], axis=0, keepdims=True)
         return carry
 
-    lax.fori_loop(0, out.shape[1] // CHUNK, step, 0)
+    lax.fori_loop(0, out.shape[1] // CHUNK, step, 0, unroll=2)
 
 
 def lines_forward(acc, c, table, send):
@@ -250,8 +250,7 @@
         for d in range(3):
             whole_gap = row[d : d + 1] - col[:, d : d + 1]
             if d > 0:
-                whole_gap = jnp.where(whole_gap > 64.0, whole_gap - 128.0, whole_gap)
-                whole_gap = jnp.where(whole_gap < -64.0, whole_gap + 128.0, whole_gap)
+                whole_gap = whole_gap - 128.0 * jnp.round(whole_gap * (1.0 / 128.0))
             gap.append(whole_gap + (row[3 + d : 4 + d] - col[:, 3 + d : 4 + d]))
         distance = gap[0] * gap[0] + gap[1] * gap[1] + gap[2] * gap[2]
         inverse = lax.rsqrt(distance + 1.0)

time: 81 us -> 78.6 us (0.970)
  Pallas kernels: 78.8 us -> 76.3 us
    pallas_call x1, Pallas kernels: 78.8 us -> 76.3 us  [step(): pl.pallas_call(step_kernel, in_specs=[vmem] * 4 + [pl.BlockSpec(memory_sp...]
where the time goes in v3:
time: 78.6 us; the launch traced here: 78.4 us
  Pallas kernels  76.3 us (97%)
  other arithmetic  1.4 us (2%)
    pallas_call x1, Pallas kernels, step(): pl.pallas_call(step_kernel, in_specs=[vmem] * 4 + [pl.BlockSpec(memory_sp...  76.3 us

profile of v3, /device:TPU:1, one launch (start us, length us, event | category | flops | bytes accessed | tf_op | source)
XLA Modules:
  0.0 78.4 jit_solution(9649187502329869764)
XLA Ops:
  0.7 76.3 %step.1 = (f32[3,2048]{1,0:T(4,128)}, f32[3,2048]{1,0:T(4,128)}) custom-call(s32[3,2048]{1,0:T(4,128)} %start.1, f32[3,2048]{1,0:T(4,128)} %fraction.1, f32[3,2048]{1,0:T(4,128)} %force.1, s32[2,48]{1,0:T(2,128)} %bitcast.1, s32[1]{0:T(128)S(6)} %copy.18.used, bf16[128,128]{1,0:T(8,128)(2,1)} %constant.24.clone.fz_high, ...), custom_call_target="tpu_custom_call" | custom-call | tf_op jit(solution)/shard_map/step/pallas_call | solution.py:483
  77.0 1.4 %add.3 = f32[3,2048]{1,0:T(4,128)} add(f32[3,2048]{1,0:T(4,128)} %get-tuple-element.7, f32[3,2048]{1,0:T(4,128)} %get-tuple-element.8) | non-fusion elementwise | flops 6144 | bytes 73728 | tf_op jit(solution)/shard_map/add | solution.py:539

commit v4 on v3

--- a/solution.py
+++ b/solution.py
@@ -443,13 +443,14 @@
 
     way_back(0)
     way_back(1)
+    way_back(2)
+    near_terms(tiles, terms, 16, 22)
     last_way(0)
-    way_back(2)
-    near_terms(tiles, terms, 16, 26)
+    near_terms(tiles, terms, 22, 30)
     last_way(1)
-    near_terms(tiles, terms, 26, 36)
+    near_terms(tiles, terms, 30, 38)
     last_way(2)
-    near_terms(tiles, terms, 36, SLOTS)
+    near_terms(tiles, terms, 38, SLOTS)
     slot = lax.broadcasted_iota(jnp.int32, slot_tile.shape, 1)
     live = jnp.where((slot_tile == pairs[0:1, :]) & (slot < used[0]), 1.0, 0.0)
     near_sum(live, terms, near)

time: 78.6 us -> 78.3 us (level)
  no operation moved by 1% of the time
where the time goes in v4:
time: 78.3 us; the launch traced here: 78.1 us
  Pallas kernels  76 us (97%)
  other arithmetic  1.4 us (2%)
    pallas_call x1, Pallas kernels, step(): pl.pallas_call(step_kernel, in_specs=[vmem] * 4 + [pl.BlockSpec(memory_sp...  76 us

profile of v4, /device:TPU:1, one launch (start us, length us, event | category | flops | bytes accessed | tf_op | source)
XLA Modules:
  0.0 78.1 jit_solution(9760230814233326112)
XLA Ops:
  0.7 76.0 %step.1 = (f32[3,2048]{1,0:T(4,128)}, f32[3,2048]{1,0:T(4,128)}) custom-call(s32[3,2048]{1,0:T(4,128)} %start.1, f32[3,2048]{1,0:T(4,128)} %fraction.1, f32[3,2048]{1,0:T(4,128)} %force.1, s32[2,48]{1,0:T(2,128)} %bitcast.1, s32[1]{0:T(128)S(6)} %copy.18.used, bf16[128,128]{1,0:T(8,128)(2,1)} %constant.24.clone.fz_high, ...), custom_call_target="tpu_custom_call" | custom-call | tf_op jit(solution)/shard_map/step/pallas_call | solution.py:484
  76.7 1.4 %add.3 = f32[3,2048]{1,0:T(4,128)} add(f32[3,2048]{1,0:T(4,128)} %get-tuple-element.7, f32[3,2048]{1,0:T(4,128)} %get-tuple-element.8) | non-fusion elementwise | flops 6144 | bytes 73728 | tf_op jit(solution)/shard_map/add | solution.py:540
